TPU v7x, 32 devices: a whole 2x2x4 slice. The times are simulated.
32 devices in a mesh: wide: 16 (over z, y, core), narrow: 2 (over x).
Axes of the slice: x: 2, y: 2, z: 4, core: 2. Of those that a mesh axis runs over, the one named last changes fastest.
Arguments:
- query_coords: float32 [3, 32, 16, 32], P(None, ('wide', 'narrow')), may hold values from -1 to 1
- owner_element: int32 [32, 16, 32], P(('wide', 'narrow')), may hold values from 0 to 15
- pair_counts: int32 [32, 32], P(('wide', 'narrow')), may hold values from 0 to 16, as said below
- fields: bfloat16 [512, 8, 1024], P(('wide', 'narrow')), may hold values from -6 to 6
Outputs:
- values: bfloat16 [16, 32, 16, 32], P(None, ('wide', 'narrow'))
Inputs may be any that keep to these rules, and one draw needn't show every extreme that they name: `pair_counts`: every count is at most 16, and some pair of devices reaches 16 in every draw.
All inputs are finite; a program needn't handle non-finite values.
Results may differ from a plain program's by a relative error of at most 0.0043.
Values may be sent and summed in bfloat16 or wider, within the bound.
No kernel may reach another device: no remote copies, remote signals or barrier semaphores. Data moves between devices by JAX's collectives and lax.ppermute only.
A program may use at most 64 MiB of HBM per device.

v0:
```python
import math

import jax
import jax.numpy as jnp
from jax import lax
from jax.sharding import PartitionSpec as P

GLL_NODES = (
    -1.0,
    -0.8717401485096066,
    -0.5917001814331423,
    -0.2092992179024789,
    0.2092992179024789,
    0.5917001814331423,
    0.8717401485096066,
    1.0,
)


def for_sending(shard):
    return jax.tree.map(lambda a: a.astype(jnp.bfloat16) if a.dtype == jnp.float32 else a, shard)


def lagrange(position):
    result = []
    for i in range(8):
        factor = jnp.ones_like(position)
        for m in range(8):
            if m != i:
                factor = factor * ((position - GLL_NODES[m]) / (GLL_NODES[i] - GLL_NODES[m]))
        result.append(factor)
    return jnp.stack(result)


def interpolate(payload, field_table):
    element_count = field_table.shape[0] // 8
    column_count = field_table.shape[1]
    half_cols = column_count // 2
    basis_r = lagrange(payload[0]).astype(jnp.bfloat16)
    tensor_st = (lagrange(payload[1])[:, None, :] * lagrange(payload[2])[None, :, :]).reshape(
        64, -1
    )
    picked = payload[3][None, :] == jnp.arange(element_count, dtype=jnp.float32)[:, None]
    weights = jnp.where(
        picked[:, None, :], basis_r[None, :, :], jnp.zeros((), jnp.bfloat16)
    ).reshape(element_count * 8, -1)
    halves = []
    for h in range(2):
        partial_value = lax.dot_general(
            field_table[:, h * half_cols : (h + 1) * half_cols],
            weights,
            (((0,), (0,)), ((), ())),
            preferred_element_type=jnp.float32,
        )
        halves.append(
            jnp.sum(partial_value.reshape(half_cols // 64, 64, -1) * tensor_st[None, :, :], axis=1)
        )
    return jnp.concatenate(halves, axis=0).astype(jnp.bfloat16)


def evaluate(payload, field_table):
    field_count = field_table.shape[1] // 64
    lead_shape = payload.shape[1:]
    flat = payload.reshape(4, -1)
    total_rows = flat.shape[1]
    block_rows = math.gcd(total_rows, 512)
    blocks = jnp.transpose(flat.reshape(4, total_rows // block_rows, block_rows), (1, 0, 2))

    def one_block(block):
        return interpolate(block, field_table)

    results = lax.map(one_block, blocks)
    return jnp.transpose(results, (1, 0, 2)).reshape((field_count,) + lead_shape)


def on_device(query_coords, owner_element, pair_counts, fields):
    wide_size = lax.axis_size("wide")
    narrow_size = lax.axis_size("narrow")
    device_count = wide_size * narrow_size
    slot_count = owner_element.shape[1]
    element_count = fields.shape[0]
    field_table = fields.reshape(element_count * fields.shape[1], fields.shape[2])
    live = jnp.arange(slot_count, dtype=jnp.int32)[:, None] < pair_counts[0][None, :]
    element_float = jnp.where(live, owner_element[0], element_count).astype(jnp.float32)
    payload = jnp.concatenate([query_coords[:, 0], element_float[None]], axis=0)
    payload = payload.reshape(4, slot_count, wide_size, narrow_size)
    arrived = lax.all_to_all(
        lax.all_to_all(payload, "wide", split_axis=2, concat_axis=2, tiled=True),
        "narrow",
        split_axis=3,
        concat_axis=3,
        tiled=True,
    )
    result = evaluate(arrived, field_table)
    returned = lax.all_to_all(
        lax.all_to_all(for_sending(result), "wide", split_axis=2, concat_axis=2, tiled=True),
        "narrow",
        split_axis=3,
        concat_axis=3,
        tiled=True,
    ).astype(result.dtype)
    return returned.reshape(returned.shape[0], 1, slot_count, device_count)


def solution(mesh):
    placed = (
        P(None, ("wide", "narrow"), None, None),
        P(("wide", "narrow"), None, None),
        P(("wide", "narrow"), None),
        P(("wide", "narrow"), None, None),
    )
    return jax.shard_map(
        on_device,
        mesh=mesh,
        in_specs=placed,
        out_specs=P(None, ("wide", "narrow"), None, None),
        check_vma=False,
    )
```

profile of v0, /device:TPU:0, one launch (start us, length us, event | category | flops | bytes accessed | tf_op | source)
XLA Modules:
  0.0 51.5 jit_solution(9558058476863743550)
XLA Ops:
  0.0 0.8 %copy.35 = s32[1,16,32]{1,2,0:T(8,128)S(1)} copy(s32[1,16,32]{2,1,0:T(8,128)} %param.5) | data formatting | bytes 4096 | tf_op args[1]
  0.9 0.7 %copy-done.2 = s32[1,32]{1,0:T(1,128)S(1)} copy-done((s32[1,32]{1,0:T(1,128)S(1)}, s32[1,32]{1,0:T(1,128)}, u32[]{:S(2)}) %copy-start.2) | copy-done | bytes 152
  1.8 13.7 %all_to_all.20 = f32[16,1,128]{2,1,0:T(1,128)S(1)} all-to-all(f32[16,1,128]{2,1,0:T(1,128)S(1)} %reshape.2410), channel_id=1, replica_groups=mesh['wide'=16,'narrow'=2] {'wide'}, dimensions={0} | all-to-all | bytes 16384 | tf_op jit(solution)/shard_map/all_to_all | solution.py:88
  15.4 0.5 broadcast.3145
  15.9 0.7 %reduce = f32[16,128]{1,0:T(8,128)S(1)} reduce(f32[16,1,128]{2,1,0:T(1,128)S(1)} %all_to_all.20, f32[]{:T(128)} %broadcast.3145), dimensions={1}, to_apply=%all_to_all.12.reduce_sub_computation | reduce | bytes 16388 | tf_op jit(solution)/shard_map/all_to_all | solution.py:88
  16.9 6.4 %all_to_all.21 = f32[2,1,1024]{2,1,0:T(1,128)S(1)} all-to-all(f32[2,1,1024]{2,1,0:T(1,128)S(1)} %reshape.2412), channel_id=1, replica_groups=mesh['wide'=16,'narrow'=2] {'narrow'}, dimensions={0} | all-to-all | bytes 16384 | tf_op jit(solution)/shard_map/all_to_all | solution.py:87
  23.2 0.7 %reduce.1 = f32[2,1024]{1,0:T(2,128)S(1)} reduce(f32[2,1,1024]{2,1,0:T(1,128)S(1)} %all_to_all.21, f32[]{:T(128)} %broadcast.3145), dimensions={1}, to_apply=%all_to_all.13.reduce_sub_computation | reduce | bytes 16388 | tf_op jit(solution)/shard_map/all_to_all | solution.py:87
  24.1 0.2 multiply_convert_fusion
  24.2 0.2 copy.38
  24.6 0.2 copy.57
  24.9 0.2 copy.55
  25.2 0.2 copy.56
  25.5 0.2 copy.62
  25.9 0.2 copy.54
  26.2 0.2 copy.46
  26.4 0.1 reshape.2409
  26.5 0.2 copy.45
  26.7 0.1 reshape.2408
  26.9 0.2 copy.44
  27.2 0.2 copy.43
  27.4 0.1 reshape.2406
  27.6 0.2 copy.42
  27.9 0.2 copy.41
  28.3 0.2 copy.39
  28.7 0.2 copy.40
  29.0 0.2 copy.53
  29.3 0.2 copy.52
  29.7 0.2 copy.51
  30.0 0.2 copy.50
  30.3 0.2 copy.49
  30.6 0.2 copy.47
  31.0 0.2 copy.48
  31.3 0.2 copy.61
  31.6 0.2 copy.60
  31.9 0.2 copy.59
  32.3 0.2 copy.58
  32.7 0.5 copy-done
  33.2 0.3 fusion
  33.5 0.4 multiply_reduce_fusion.1
  33.9 0.2 copy.63
  34.1 0.2 copy.64
  34.2 0.4 copy_bitcast_fusion.1
  34.6 0.2 reshape.2414
  34.8 9.1 %all_to_all.22 = bf16[16,2,256]{2,1,0:T(2,128)(2,1)S(1)} all-to-all(bf16[16,2,256]{2,1,0:T(2,128)(2,1)S(1)} %reshape.2414), channel_id=1, replica_groups=mesh['wide'=16,'narrow'=2] {'wide'}, dimensions={0} | all-to-all | bytes 32768 | tf_op jit(solution)/shard_map/all_to_all | solution.py:96
  44.0 0.2 reshape.2416
  44.2 6.2 %all_to_all.23 = bf16[2,2,2048]{2,1,0:T(2,128)(2,1)S(1)} all-to-all(bf16[2,2,2048]{2,1,0:T(2,128)(2,1)S(1)} %reshape.2416), channel_id=1, replica_groups=mesh['wide'=16,'narrow'=2] {'narrow'}, dimensions={0} | all-to-all | bytes 32768 | tf_op jit(solution)/shard_map/all_to_all | solution.py:95
  50.6 0.2 copy.67
  50.7 0.8 %copy.68 = bf16[16,1,16,32]{3,2,1,0:T(8,128)(2,1)} copy(bf16[16,1,16,32]{2,0,3,1:T(8,128)(2,1)S(1)} %bitcast.93) | data formatting | bytes 32768 | tf_op jit(solution)/shard_map/reshape | solution.py:102
  (43 shorter events, 4.3 us)
Async XLA Ops:
  0.0 0.8 %copy-start.1 = (f32[3,1,16,32]{3,2,1,0:T(8,128)S(1)}, f32[3,1,16,32]{3,2,1,0:T(8,128)}, u32[]{:S(2)}) copy-start(f32[3,1,16,32]{3,2,1,0:T(8,128)} %param.4) | copy-start | bytes 18436
  0.9 0.7 %copy-start.2 = (s32[1,32]{1,0:T(1,128)S(1)}, s32[1,32]{1,0:T(1,128)}, u32[]{:S(2)}) copy-start(s32[1,32]{1,0:T(1,128)} %param.6) | copy-start | bytes 388
  32.3 1.0 %copy-start = (bf16[16,8,1024]{2,1,0:T(8,128)(2,1)S(1)}, bf16[16,8,1024]{2,1,0:T(8,128)(2,1)}, u32[]{:S(2)}) copy-start(bf16[16,8,1024]{2,1,0:T(8,128)(2,1)} %param.7) | copy-start | bytes 786436
where the time goes:
time: 51.9 us; the launch traced here: 51.5 us
  blocking collectives  35.3 us (68%)
  local copies, waits for them, and re-layouts  13.2 us (25%)
  other arithmetic  2.05 us (4%)
  matrix products  0.69 us (1%)
    all_to_all x1, blocking collectives, on_device(): lax.all_to_all(payload, 'wide', split_axis=2, concat_axis=2, tiled=True)  13.7 us
    all_to_all x1, blocking collectives, on_device(): lax.all_to_all(for_sending(result), 'wide', split_axis=2, concat_axis=2,...  9.07 us
    all_to_all x1, blocking collectives, on_device(): lax.all_to_all(lax.all_to_all(payload, 'wide', split_axis=2, concat_axis=...  6.37 us
    all_to_all x1, blocking collectives, on_device(): lax.all_to_all(lax.all_to_all(for_sending(result), 'wide', split_axis=2,...  6.2 us
    mul x32, local copies, waits for them, and re-layouts, lagrange(): factor * ((position - GLL_NODES[m]) / (GLL_NODES[i] - GLL_NODES[m]))  5.1 us
    another operation x18, local copies, waits for them, and re-layouts  3.09 us
    unnamed x16, local copies, waits for them, and re-layouts  3.02 us

commit v1 on v0

v1 whole, which is shorter than its diff:
```python
import functools
import math

import jax
import jax.numpy as jnp
from jax import lax
from jax.experimental import pallas as pl
from jax.experimental.pallas import tpu as pltpu
from jax.sharding import PartitionSpec as P

GLL_NODES = (
    -1.0,
    -0.8717401485096066,
    -0.5917001814331423,
    -0.2092992179024789,
    0.2092992179024789,
    0.5917001814331423,
    0.8717401485096066,
    1.0,
)
NODE_COUNT = len(GLL_NODES)
SCALES = tuple(
    1.0 / math.prod(GLL_NODES[i] - GLL_NODES[m] for m in range(NODE_COUNT) if m != i)
    for i in range(NODE_COUNT)
)
AXES = ("wide", "narrow")
LANES = 128
ROWS = 8


def lagrange(position):
    node = lax.broadcasted_iota(jnp.int32, (NODE_COUNT, position.shape[1]), 0)
    result = jnp.full(node.shape, SCALES[0], jnp.float32)
    for i in range(1, NODE_COUNT):
        result = jnp.where(node == i, SCALES[i], result)
    for m in range(NODE_COUNT):
        result = result * jnp.where(node == m, 1.0, position - GLL_NODES[m])
    return result


def pack_kernel(coords_ref, element_ref, counts_ref, out_ref, *, element_count):
    slots, devices = element_ref.shape
    slot = lax.broadcasted_iota(jnp.int32, (slots, devices), 0)
    element = jnp.where(slot < counts_ref[...], element_ref[...], element_count)
    rows = jnp.concatenate(
        [
            coords_ref[...].reshape(3 * slots, devices),
            element.astype(jnp.float32),
            jnp.zeros(((ROWS - 4) * slots, devices), jnp.float32),
        ],
        axis=0,
    )
    out_ref[...] = rows.T


def evaluate_kernel(query_ref, fields_ref, out_ref, query_rows, result_rows, *, slots):
    senders = query_ref.shape[0]
    points = senders * slots
    table_rows, columns = fields_ref.shape
    element_count = table_rows // NODE_COUNT
    pairs = NODE_COUNT * NODE_COUNT
    field_count = columns // pairs
    query_rows[:, :senders] = query_ref[...].T
    query = jnp.concatenate(
        [query_rows[pl.ds(k, ROWS, stride=slots), :senders] for k in range(slots)], axis=1
    )
    basis_r = lagrange(query[0:1]).astype(jnp.bfloat16).astype(jnp.float32)
    basis_s = lagrange(query[1:2])
    basis_t = lagrange(query[2:3])
    element = query[3:4]
    weights = jnp.concatenate(
        [jnp.where(element == float(e), basis_r, 0.0) for e in range(element_count)], axis=0
    ).astype(jnp.bfloat16)
    tensor_st = jnp.concatenate(
        [basis_s[j : j + 1] * basis_t for j in range(NODE_COUNT)], axis=0
    )
    partial = lax.dot_general(
        fields_ref[...],
        weights,
        (((0,), (0,)), ((), ())),
        preferred_element_type=jnp.float32,
    )
    values = jnp.sum(
        partial.reshape(field_count, pairs, points) * tensor_st[None, :, :], axis=1
    )
    for k in range(slots):
        start = k * senders
        tile = values[:, start // LANES * LANES : start // LANES * LANES + LANES]
        shift = start % LANES
        if shift:
            tile = pltpu.roll(tile, LANES - shift, 1)
        result_rows[pl.ds(k, field_count, stride=slots), :] = tile
    out_ref[...] = result_rows[...].T[:senders].astype(jnp.bfloat16)


def unpack_kernel(result_ref, out_ref):
    out_ref[...] = (
        result_ref[...].astype(jnp.float32).T.reshape(out_ref.shape).astype(jnp.bfloat16)
    )


def exchange(array):
    return lax.all_to_all(array, AXES, split_axis=0, concat_axis=0, tiled=True)


def on_device(query_coords, owner_element, pair_counts, fields):
    device_count = lax.axis_size("wide") * lax.axis_size("narrow")
    slots = owner_element.shape[1]
    element_count, node_count, columns = fields.shape
    field_count = columns // (node_count * node_count)
    field_table = fields.reshape(element_count * node_count, columns)
    sent = pl.pallas_call(
        functools.partial(pack_kernel, element_count=element_count),
        out_shape=jax.ShapeDtypeStruct((device_count, ROWS * slots), jnp.float32),
        name="pack",
    )(query_coords[:, 0], owner_element[0], pair_counts)
    arrived = exchange(sent)
    senders = math.gcd(device_count, 32)
    result = pl.pallas_call(
        functools.partial(evaluate_kernel, slots=slots),
        out_shape=jax.ShapeDtypeStruct((device_count, field_count * slots), jnp.bfloat16),
        grid=(device_count // senders,),
        in_specs=[
            pl.BlockSpec((senders, ROWS * slots), lambda b: (b, 0)),
            pl.BlockSpec(field_table.shape, lambda b: (0, 0)),
        ],
        out_specs=pl.BlockSpec((senders, field_count * slots), lambda b: (b, 0)),
        scratch_shapes=[
            pltpu.VMEM((ROWS * slots, LANES), jnp.float32),
            pltpu.VMEM((field_count * slots, LANES), jnp.float32),
        ],
        name="evaluate",
    )(arrived, field_table)
    returned = exchange(result)
    values = pl.pallas_call(
        unpack_kernel,
        out_shape=jax.ShapeDtypeStruct((field_count, slots, device_count), jnp.bfloat16),
        name="unpack",
    )(returned)
    return values[:, None]


def solution(mesh):
    placed = (
        P(None, AXES, None, None),
        P(AXES, None, None),
        P(AXES, None),
        P(AXES, None, None),
    )
    return jax.shard_map(
        on_device,
        mesh=mesh,
        in_specs=placed,
        out_specs=P(None, AXES, None, None),
        check_vma=False,
    )
```

time: 51.9 us -> 31.8 us (0.61)
  local copies, waits for them, and re-layouts: 13.2 us -> 1.22 us
  blocking collectives: 35.3 us -> 23.4 us
  Pallas kernels: 0 us -> 5.29 us
  matrix products: 0.69 us -> 0 us
  other arithmetic: 2.05 us -> 1.41 us
    all_to_all x4 -> x2, blocking collectives: 35.3 us -> 23.4 us  [exchange(): return lax.all_to_all(array, AXES, split_axis=0, concat_axis=0, tiled=True)]
    pallas_call x0 -> x3, Pallas kernels: none -> 5.29 us  [the longest x1 2.4 us: on_device(): pl.pallas_call(functools.partial(evaluate_kernel, slots=slots), out_shape...]
    mul x32 -> x0, local copies, waits for them, and re-layouts: 5.1 us -> none  [lagrange(): factor * ((position - GLL_NODES[m]) / (GLL_NODES[i] - GLL_NODES[m]))]
    another operation x21 -> x0, local copies, waits for them, and re-layouts: 3.21 us -> none
    unnamed x16 -> x3, local copies, waits for them, and re-layouts: 3.02 us -> 0.63 us
    reshape x1 -> x0, local copies, waits for them, and re-layouts: 0.8 us -> none  [on_device(): return returned.reshape(returned.shape[0], 1, slot_count, device_count)]
    dot_general x2 -> x0, matrix products: 0.69 us -> none  [interpolate(): lax.dot_general(field_table[:, h * half_cols:(h + 1) * half_cols], weight...]
    all_to_all x2 -> x1, other arithmetic: 1.34 us -> 1.41 us  [exchange(): return lax.all_to_all(array, AXES, split_axis=0, concat_axis=0, tiled=True)]
where the time goes in v1:
time: 31.8 us; the launch traced here: 31.3 us
  blocking collectives  23.4 us (74%)
  Pallas kernels  5.29 us (17%)
  other arithmetic  1.41 us (4%)
  local copies, waits for them, and re-layouts  1.22 us (4%)
    all_to_all x2, blocking collectives, exchange(): return lax.all_to_all(array, AXES, split_axis=0, concat_axis=0, tiled=True)  23.4 us
    pallas_call x1, Pallas kernels, on_device(): pl.pallas_call(functools.partial(evaluate_kernel, slots=slots), out_shape...  2.4 us
    pallas_call x1, Pallas kernels, on_device(): pl.pallas_call(unpack_kernel, out_shape=jax.ShapeDtypeStruct((field_count...  1.45 us
    pallas_call x1, Pallas kernels, on_device(): pl.pallas_call(functools.partial(pack_kernel, element_count=element_count...  1.43 us
    all_to_all x1, other arithmetic, exchange(): return lax.all_to_all(array, AXES, split_axis=0, concat_axis=0, tiled=True)  1.41 us

profile of v1, /device:TPU:0, one launch (start us, length us, event | category | flops | bytes accessed | tf_op | source)
XLA Modules:
  0.0 31.3 jit_solution(11207305002220781126)
XLA Ops:
  0.0 1.4 %pack.1 = f32[32,128]{1,0:T(8,128)} custom-call(f32[3,16,32]{2,1,0:T(8,128)} %bitcast.19, s32[16,32]{1,0:T(8,128)} %bitcast.20, s32[1,32]{1,0:T(1,128)} %counts_ref.1), custom_call_target="tpu_custom_call" | custom-call | tf_op jit(solution)/shard_map/pack/pallas_call | solution.py:112
  1.4 14.5 %all_to_all.22 = f32[32,1,128]{2,1,0:T(1,128)} all-to-all(f32[32,1,128]{2,1,0:T(1,128)} %bitcast.18), channel_id=1, replica_groups=mesh['wide'=16,'narrow'=2] {'wide','narrow'}, dimensions={0} | all-to-all | bytes 32768 | tf_op jit(solution)/shard_map/all_to_all | solution.py:103
  15.9 2.4 %evaluate.1 = bf16[32,256]{1,0:T(8,128)(2,1)} custom-call(f32[32,128]{1,0:T(8,128)} %bitcast.17, bf16[128,1024]{1,0:T(8,128)(2,1)} %bitcast.14), custom_call_target="tpu_custom_call" | custom-call | tf_op jit(solution)/shard_map/evaluate/pallas_call | solution.py:119
  18.3 0.6 %broadcast = bf16[]{:T(256)} broadcast(bf16[]{:T(256)} %constant.4), dimensions={} | broadcast | bytes 4 | tf_op jit(solution)/shard_map/all_to_all | solution.py:103
  18.9 1.4 %reduce = bf16[32,256]{1,0:T(8,128)(2,1)S(1)} reduce(bf16[32,1,256]{2,0,1:T(8,128)(2,1)} %bitcast.16, bf16[]{:T(256)} %broadcast), dimensions={1}, to_apply=%copy.10.reduce_sub_computation | reduce | bytes 32770 | tf_op jit(solution)/shard_map/all_to_all | solution.py:103
  20.3 8.9 %all_to_all.23 = bf16[32,2,128]{2,1,0:T(2,128)(2,1)S(1)} all-to-all(bf16[32,2,128]{2,1,0:T(2,128)(2,1)S(1)} %reshape.8), channel_id=1, replica_groups=mesh['wide'=16,'narrow'=2] {'wide','narrow'}, dimensions={0} | all-to-all | bytes 32768 | tf_op jit(solution)/shard_map/all_to_all | solution.py:103
  29.3 0.6 %copy.14 = bf16[32,1,256]{2,0,1:T(8,128)(2,1)} copy(bf16[32,1,256]{2,1,0:T(2,128)(2,1)S(1)} %reshape.9) | data formatting | bytes 32768
  29.9 1.4 %unpack.1 = bf16[16,16,32]{2,1,0:T(8,128)(2,1)} custom-call(bf16[32,256]{1,0:T(8,128)(2,1)} %bitcast.15), custom_call_target="tpu_custom_call" | custom-call | tf_op jit(solution)/shard_map/unpack/pallas_call | solution.py:135
  (2 shorter events, 0.0 us)

commit v2 on v1

--- a/solution.py
+++ b/solution.py
@@ -53,7 +53,9 @@
     out_ref[...] = rows.T
 
 
-def evaluate_kernel(query_ref, fields_ref, out_ref, query_rows, result_rows, *, slots):
+def evaluate_kernel(
+    query_ref, fields_ref, out_ref, query_rows, result_rows, sent_rows, *, slots
+):
     senders = query_ref.shape[0]
     points = senders * slots
     table_rows, columns = fields_ref.shape
@@ -90,13 +92,24 @@
         if shift:
             tile = pltpu.roll(tile, LANES - shift, 1)
         result_rows[pl.ds(k, field_count, stride=slots), :] = tile
-    out_ref[...] = result_rows[...].T[:senders].astype(jnp.bfloat16)
+    pieces = field_count * slots // LANES
+    for piece in range(pieces):
+        sent_rows[pl.ds(piece, senders, stride=pieces), :] = result_rows[
+            piece * LANES : (piece + 1) * LANES, :
+        ].T[:senders]
+    out_ref[...] = sent_rows[...].astype(jnp.bfloat16)
 
 
-def unpack_kernel(result_ref, out_ref):
-    out_ref[...] = (
-        result_ref[...].astype(jnp.float32).T.reshape(out_ref.shape).astype(jnp.bfloat16)
-    )
+def unpack_kernel(result_ref, out_ref, arrived_rows):
+    field_count, slots, devices = out_ref.shape
+    pieces = field_count * slots // LANES
+    share = field_count // pieces
+    arrived_rows[...] = result_ref[...].astype(jnp.float32)
+    for piece in range(pieces):
+        rows = arrived_rows[pl.ds(piece, devices, stride=pieces), :].T
+        out_ref[piece * share : (piece + 1) * share] = rows.reshape(
+            share, slots, devices
+        ).astype(jnp.bfloat16)
 
 
 def exchange(array):
@@ -116,18 +129,20 @@
     )(query_coords[:, 0], owner_element[0], pair_counts)
     arrived = exchange(sent)
     senders = math.gcd(device_count, 32)
+    pieces = field_count * slots // LANES
     result = pl.pallas_call(
         functools.partial(evaluate_kernel, slots=slots),
-        out_shape=jax.ShapeDtypeStruct((device_count, field_count * slots), jnp.bfloat16),
+        out_shape=jax.ShapeDtypeStruct((device_count * pieces, LANES), jnp.bfloat16),
         grid=(device_count // senders,),
         in_specs=[
             pl.BlockSpec((senders, ROWS * slots), lambda b: (b, 0)),
             pl.BlockSpec(field_table.shape, lambda b: (0, 0)),
         ],
-        out_specs=pl.BlockSpec((senders, field_count * slots), lambda b: (b, 0)),
+        out_specs=pl.BlockSpec((senders * pieces, LANES), lambda b: (b, 0)),
         scratch_shapes=[
             pltpu.VMEM((ROWS * slots, LANES), jnp.float32),
             pltpu.VMEM((field_count * slots, LANES), jnp.float32),
+            pltpu.VMEM((senders * pieces, LANES), jnp.float32),
         ],
         name="evaluate",
     )(arrived, field_table)
@@ -135,6 +150,7 @@
     values = pl.pallas_call(
         unpack_kernel,
         out_shape=jax.ShapeDtypeStruct((field_count, slots, device_count), jnp.bfloat16),
+        scratch_shapes=[pltpu.VMEM((device_count * pieces, LANES), jnp.float32)],
         name="unpack",
     )(returned)
     return values[:, None]

time: 31.8 us -> 30.4 us (0.956)
  other arithmetic: 1.41 us -> 0 us
  blocking collectives: 23.4 us -> 24.7 us
  local copies, waits for them, and re-layouts: 1.22 us -> 0 us
    all_to_all x1 -> x0, other arithmetic: 1.41 us -> none  [exchange(): return lax.all_to_all(array, AXES, split_axis=0, concat_axis=0, tiled=True)]
    all_to_all x2, blocking collectives: 23.4 us -> 24.7 us  [exchange(): return lax.all_to_all(array, AXES, split_axis=0, concat_axis=0, tiled=True)]
    unnamed x3 -> x0, local copies, waits for them, and re-layouts: 0.63 us -> none
    all_to_all x1 -> x0, local copies, waits for them, and re-layouts: 0.59 us -> none  [exchange(): return lax.all_to_all(array, AXES, split_axis=0, concat_axis=0, tiled=True)]
where the time goes in v2:
time: 30.4 us; the launch traced here: 30 us
  blocking collectives  24.7 us (81%)
  Pallas kernels  5.3 us (17%)
    all_to_all x2, blocking collectives, exchange(): return lax.all_to_all(array, AXES, split_axis=0, concat_axis=0, tiled=True)  24.7 us
    pallas_call x1, Pallas kernels, on_device(): pl.pallas_call(functools.partial(evaluate_kernel, slots=slots), out_shape...  2.41 us
    pallas_call x1, Pallas kernels, on_device(): pl.pallas_call(unpack_kernel, out_shape=jax.ShapeDtypeStruct((field_count...  1.46 us
    pallas_call x1, Pallas kernels, on_device(): pl.pallas_call(functools.partial(pack_kernel, element_count=element_count...  1.43 us

profile of v2, /device:TPU:0, one launch (start us, length us, event | category | flops | bytes accessed | tf_op | source)
XLA Modules:
  0.0 30.0 jit_solution(15169087270798700985)
XLA Ops:
  0.0 1.4 %pack.1 = f32[32,128]{1,0:T(8,128)} custom-call(f32[3,16,32]{2,1,0:T(8,128)} %bitcast.17, s32[16,32]{1,0:T(8,128)} %bitcast.18, s32[1,32]{1,0:T(1,128)} %counts_ref.1), custom_call_target="tpu_custom_call" | custom-call | tf_op jit(solution)/shard_map/pack/pallas_call | solution.py:125
  1.4 14.5 %all_to_all.22 = f32[32,1,128]{2,1,0:T(1,128)} all-to-all(f32[32,1,128]{2,1,0:T(1,128)} %bitcast.16), channel_id=1, replica_groups=mesh['wide'=16,'narrow'=2] {'wide','narrow'}, dimensions={0} | all-to-all | bytes 32768 | tf_op jit(solution)/shard_map/all_to_all | solution.py:116
  15.9 2.4 %evaluate.1 = bf16[64,128]{1,0:T(8,128)(2,1)} custom-call(f32[32,128]{1,0:T(8,128)} %bitcast.13, bf16[128,1024]{1,0:T(8,128)(2,1)} %bitcast.12), custom_call_target="tpu_custom_call" | custom-call | tf_op jit(solution)/shard_map/evaluate/pallas_call | solution.py:133
  18.3 10.3 %all_to_all.23 = bf16[32,2,128]{2,1,0:T(2,128)(2,1)} all-to-all(bf16[32,2,128]{2,1,0:T(2,128)(2,1)} %bitcast.14), channel_id=1, replica_groups=mesh['wide'=16,'narrow'=2] {'wide','narrow'}, dimensions={0} | all-to-all | bytes 32768 | tf_op jit(solution)/shard_map/all_to_all | solution.py:116
  28.6 1.5 %unpack.1 = bf16[16,16,32]{2,1,0:T(8,128)(2,1)} custom-call(bf16[64,128]{1,0:T(8,128)(2,1)} %bitcast.15), custom_call_target="tpu_custom_call" | custom-call | tf_op jit(solution)/shard_map/unpack/pallas_call | solution.py:150

commit v3 on v2

v3 whole, which is shorter than its diff:
```python
import functools
import math

import jax
import jax.numpy as jnp
from jax import lax
from jax.experimental import pallas as pl
from jax.experimental.pallas import tpu as pltpu
from jax.sharding import PartitionSpec as P

GLL_NODES = (
    -1.0,
    -0.8717401485096066,
    -0.5917001814331423,
    -0.2092992179024789,
    0.2092992179024789,
    0.5917001814331423,
    0.8717401485096066,
    1.0,
)
NODE_COUNT = len(GLL_NODES)
SCALES = tuple(
    1.0 / math.prod(GLL_NODES[i] - GLL_NODES[m] for m in range(NODE_COUNT) if m != i)
    for i in range(NODE_COUNT)
)
AXES = ("wide", "narrow")
LANES = 128
ROWS = 8
TABLE_COPIES = 8


def lagrange(position):
    node = lax.broadcasted_iota(jnp.int32, (NODE_COUNT, position.shape[1]), 0)
    result = jnp.full(node.shape, SCALES[0], jnp.float32)
    for i in range(1, NODE_COUNT):
        result = jnp.where(node == i, SCALES[i], result)
    for m in range(NODE_COUNT):
        result = result * jnp.where(node == m, 1.0, position - GLL_NODES[m])
    return result


def pack_kernel(
    coords_hbm,
    element_hbm,
    counts_hbm,
    fields_hbm,
    out_ref,
    table_ref,
    coords_ref,
    element_ref,
    counts_ref,
    input_semaphores,
    table_semaphores,
    *,
    element_count,
):
    pairs = ((coords_hbm, coords_ref), (element_hbm, element_ref), (counts_hbm, counts_ref))
    input_copies = [
        pltpu.make_async_copy(source, target, input_semaphores.at[i])
        for i, (source, target) in enumerate(pairs)
    ]
    share = table_ref.shape[0] // TABLE_COPIES
    table_copies = [
        pltpu.make_async_copy(
            fields_hbm.at[pl.ds(i * share, share), :],
            table_ref.at[pl.ds(i * share, share), :],
            table_semaphores.at[i],
        )
        for i in range(TABLE_COPIES)
    ]
    for copy in input_copies + table_copies:
        copy.start()
    for copy in input_copies:
        copy.wait()
    slots, devices = element_ref.shape
    slot = lax.broadcasted_iota(jnp.int32, (slots, devices), 0)
    element = jnp.where(slot < counts_ref[...], element_ref[...], element_count)
    rows = jnp.concatenate(
        [
            coords_ref[...].reshape(3 * slots, devices),
            element.astype(jnp.float32),
            jnp.zeros(((ROWS - 4) * slots, devices), jnp.float32),
        ],
        axis=0,
    )
    out_ref[...] = rows.T
    for copy in table_copies:
        copy.wait()


def evaluate_kernel(
    query_ref, fields_ref, out_ref, query_rows, result_rows, sent_rows, *, senders, slots
):
    points = senders * slots
    table_rows, columns = fields_ref.shape
    element_count = table_rows // NODE_COUNT
    pairs = NODE_COUNT * NODE_COUNT
    field_count = columns // pairs

    def one_block(first):
        query_rows[:, :senders] = query_ref[pl.ds(first, senders), :].T
        query = jnp.concatenate(
            [query_rows[pl.ds(k, ROWS, stride=slots), :senders] for k in range(slots)], axis=1
        )
        basis_r = lagrange(query[0:1]).astype(jnp.bfloat16).astype(jnp.float32)
        basis_s = lagrange(query[1:2])
        basis_t = lagrange(query[2:3])
        element = query[3:4]
        weights = jnp.concatenate(
            [jnp.where(element == float(e), basis_r, 0.0) for e in range(element_count)], axis=0
        ).astype(jnp.bfloat16)
        tensor_st = jnp.concatenate(
            [basis_s[j : j + 1] * basis_t for j in range(NODE_COUNT)], axis=0
        )
        partial = lax.dot_general(
            fields_ref[...],
            weights,
            (((0,), (0,)), ((), ())),
            preferred_element_type=jnp.float32,
        )
        values = jnp.sum(
            partial.reshape(field_count, pairs, points) * tensor_st[None, :, :], axis=1
        )
        for k in range(slots):
            start = k * senders
            tile = values[:, start // LANES * LANES : start // LANES * LANES + LANES]
            shift = start % LANES
            if shift:
                tile = pltpu.roll(tile, LANES - shift, 1)
            result_rows[pl.ds(k, field_count, stride=slots), :] = tile
        pieces = field_count * slots // LANES
        for piece in range(pieces):
            sent_rows[pl.ds(piece, senders, stride=pieces), :] = result_rows[
                piece * LANES : (piece + 1) * LANES, :
            ].T[:senders]
        out_ref[pl.ds(first * pieces, senders * pieces), :] = sent_rows[...].astype(jnp.bfloat16)

    if query_ref.shape[0] == senders:
        one_block(0)
    else:

        @pl.loop(0, query_ref.shape[0] // senders)
        def _(block):
            one_block(pl.multiple_of(block * senders, senders))


def unpack_kernel(result_ref, out_ref, arrived_rows):
    field_count, slots, devices = out_ref.shape
    pieces = field_count * slots // LANES
    share = field_count // pieces
    arrived_rows[...] = result_ref[...].astype(jnp.float32)
    for piece in range(pieces):
        rows = arrived_rows[pl.ds(piece, devices, stride=pieces), :].T
        out_ref[piece * share : (piece + 1) * share] = rows.reshape(
            share, slots, devices
        ).astype(jnp.bfloat16)


def exchange(array):
    return lax.all_to_all(array, AXES, split_axis=0, concat_axis=0, tiled=True)


def in_vmem(array):
    return pltpu.with_memory_space_constraint(array, pltpu.VMEM)


def on_device(query_coords, owner_element, pair_counts, fields):
    device_count = lax.axis_size("wide") * lax.axis_size("narrow")
    slots = owner_element.shape[1]
    element_count, node_count, columns = fields.shape
    field_count = columns // (node_count * node_count)
    field_table = fields.reshape(element_count * node_count, columns)
    on_chip = pl.BlockSpec(memory_space=pltpu.VMEM)
    queries = (query_coords[:, 0], owner_element[0], pair_counts)
    sent, table = pl.pallas_call(
        functools.partial(pack_kernel, element_count=element_count),
        out_shape=(
            pltpu.VMEM((device_count, ROWS * slots), jnp.float32),
            pltpu.VMEM(field_table.shape, field_table.dtype),
        ),
        in_specs=[pl.BlockSpec(memory_space=pl.ANY)] * 4,
        out_specs=(on_chip, on_chip),
        scratch_shapes=[
            *(pltpu.VMEM(array.shape, array.dtype) for array in queries),
            pltpu.SemaphoreType.DMA((len(queries),)),
            pltpu.SemaphoreType.DMA((TABLE_COPIES,)),
        ],
        name="pack",
    )(*queries, field_table)
    arrived = exchange(sent)
    senders = math.gcd(device_count, 32)
    pieces = field_count * slots // LANES
    result = pl.pallas_call(
        functools.partial(evaluate_kernel, senders=senders, slots=slots),
        out_shape=pltpu.VMEM((device_count * pieces, LANES), jnp.bfloat16),
        in_specs=[on_chip, on_chip],
        out_specs=on_chip,
        scratch_shapes=[
            pltpu.VMEM((ROWS * slots, LANES), jnp.float32),
            pltpu.VMEM((field_count * slots, LANES), jnp.float32),
            pltpu.VMEM((senders * pieces, LANES), jnp.float32),
        ],
        name="evaluate",
    )(in_vmem(arrived), in_vmem(table))
    returned = exchange(result)
    values = pl.pallas_call(
        unpack_kernel,
        out_shape=jax.ShapeDtypeStruct((field_count, slots, device_count), jnp.bfloat16),
        in_specs=[on_chip],
        out_specs=on_chip,
        scratch_shapes=[pltpu.VMEM((device_count * pieces, LANES), jnp.float32)],
        name="unpack",
    )(in_vmem(returned))
    return values[:, None]


def solution(mesh):
    placed = (
        P(None, AXES, None, None),
        P(AXES, None, None),
        P(AXES, None),
        P(AXES, None, None),
    )
    return jax.shard_map(
        on_device,
        mesh=mesh,
        in_specs=placed,
        out_specs=P(None, AXES, None, None),
        check_vma=False,
    )
```

time: 30.4 us -> 26.1 us (0.86)
  Pallas kernels: 5.3 us -> 2.56 us
  blocking collectives: 24.7 us -> 23.3 us
    pallas_call x1, Pallas kernels: 2.41 us -> 0.81 us  [on_device(): pl.pallas_call(functools.partial(evaluate_kernel, senders=senders, slots=...]
    all_to_all x2, blocking collectives: 24.7 us -> 23.3 us  [exchange(): return lax.all_to_all(array, AXES, split_axis=0, concat_axis=0, tiled=True)]
    pallas_call x1, Pallas kernels: 1.46 us -> 0.74 us  [on_device(): pl.pallas_call(unpack_kernel, out_shape=jax.ShapeDtypeStruct((field_count...]
    pallas_call x1, Pallas kernels: 1.43 us -> 1 us  [on_device(): pl.pallas_call(functools.partial(pack_kernel, element_count=element_count...]
where the time goes in v3:
time: 26.1 us; the launch traced here: 25.9 us
  blocking collectives  23.3 us (89%)
  Pallas kernels  2.56 us (10%)
    all_to_all x2, blocking collectives, exchange(): return lax.all_to_all(array, AXES, split_axis=0, concat_axis=0, tiled=True)  23.3 us
    pallas_call x1, Pallas kernels, on_device(): pl.pallas_call(functools.partial(pack_kernel, element_count=element_count...  1 us
    pallas_call x1, Pallas kernels, on_device(): pl.pallas_call(functools.partial(evaluate_kernel, senders=senders, slots=...  0.81 us
    pallas_call x1, Pallas kernels, on_device(): pl.pallas_call(unpack_kernel, out_shape=jax.ShapeDtypeStruct((field_count...  0.74 us

profile of v3, /device:TPU:0, one launch (start us, length us, event | category | flops | bytes accessed | tf_op | source)
XLA Modules:
  0.0 25.9 jit_solution(2132082847460052839)
XLA Ops:
  0.0 1.0 %pack.1 = (f32[32,128]{1,0:T(8,128)S(1)}, bf16[128,1024]{1,0:T(8,128)(2,1)S(1)}) custom-call(f32[3,16,32]{2,1,0:T(8,128)} %bitcast.17, s32[16,32]{1,0:T(8,128)} %bitcast.18, s32[1,32]{1,0:T(1,128)} %counts_hbm.1, bf16[128,1024]{1,0:T(8,128)(2,1)} %bitcast.16), custom_call_target="tpu_custom_call" | custom-call | tf_op jit(solution)/shard_map/pack/pallas_call | solution.py:175
  1.0 14.4 %all_to_all.22 = f32[32,1,128]{2,1,0:T(1,128)S(1)} all-to-all(f32[32,1,128]{2,1,0:T(1,128)S(1)} %bitcast.15), channel_id=1, replica_groups=mesh['wide'=16,'narrow'=2] {'wide','narrow'}, dimensions={0} | all-to-all | bytes 32768 | tf_op jit(solution)/shard_map/all_to_all | solution.py:160
  15.4 0.8 %evaluate.1 = bf16[64,128]{1,0:T(8,128)(2,1)S(1)} custom-call(f32[32,128]{1,0:T(8,128)S(1)} %bitcast.12, bf16[128,1024]{1,0:T(8,128)(2,1)S(1)} %get-tuple-element.8.fields_ref), custom_call_target="tpu_custom_call" | custom-call | tf_op jit(solution)/shard_map/evaluate/pallas_call | solution.py:193
  16.2 8.9 %all_to_all.23 = bf16[32,2,128]{2,1,0:T(2,128)(2,1)S(1)} all-to-all(bf16[32,2,128]{2,1,0:T(2,128)(2,1)S(1)} %bitcast.13), channel_id=1, replica_groups=mesh['wide'=16,'narrow'=2] {'wide','narrow'}, dimensions={0} | all-to-all | bytes 32768 | tf_op jit(solution)/shard_map/all_to_all | solution.py:160
  25.1 0.7 %unpack.1 = bf16[16,16,32]{2,1,0:T(8,128)(2,1)} custom-call(bf16[64,128]{1,0:T(8,128)(2,1)S(1)} %bitcast.14), custom_call_target="tpu_custom_call" | custom-call | tf_op jit(solution)/shard_map/unpack/pallas_call | solution.py:206

commit v4 on v3

--- a/solution.py
+++ b/solution.py
@@ -144,16 +144,22 @@
             one_block(pl.multiple_of(block * senders, senders))
 
 
-def unpack_kernel(result_ref, out_ref, arrived_rows):
-    field_count, slots, devices = out_ref.shape
+def unpack_kernel(result_ref, out_hbm, arrived_rows, values, semaphores):
+    field_count, slots, devices = out_hbm.shape
     pieces = field_count * slots // LANES
     share = field_count // pieces
     arrived_rows[...] = result_ref[...].astype(jnp.float32)
+    copies = []
     for piece in range(pieces):
         rows = arrived_rows[pl.ds(piece, devices, stride=pieces), :].T
-        out_ref[piece * share : (piece + 1) * share] = rows.reshape(
-            share, slots, devices
-        ).astype(jnp.bfloat16)
+        part = pl.ds(piece * share, share)
+        values[part] = rows.reshape(share, slots, devices).astype(jnp.bfloat16)
+        copies.append(
+            pltpu.make_async_copy(values.at[part], out_hbm.at[part], semaphores.at[piece])
+        )
+        copies[-1].start()
+    for copy in copies:
+        copy.wait()
 
 
 def exchange(array):
@@ -207,8 +213,12 @@
         unpack_kernel,
         out_shape=jax.ShapeDtypeStruct((field_count, slots, device_count), jnp.bfloat16),
         in_specs=[on_chip],
-        out_specs=on_chip,
-        scratch_shapes=[pltpu.VMEM((device_count * pieces, LANES), jnp.float32)],
+        out_specs=pl.BlockSpec(memory_space=pl.ANY),
+        scratch_shapes=[
+            pltpu.VMEM((device_count * pieces, LANES), jnp.float32),
+            pltpu.VMEM((field_count, slots, device_count), jnp.bfloat16),
+            pltpu.SemaphoreType.DMA((pieces,)),
+        ],
         name="unpack",
     )(in_vmem(returned))
     return values[:, None]

time: 26.1 us -> 26.1 us (level)
  no operation moved by 1% of the time
where the time goes in v4:
time: 26.1 us; the launch traced here: 25.9 us
  blocking collectives  23.3 us (89%)
  Pallas kernels  2.57 us (10%)
    all_to_all x2, blocking collectives, exchange(): return lax.all_to_all(array, AXES, split_axis=0, concat_axis=0, tiled=True)  23.3 us
    pallas_call x1, Pallas kernels, on_device(): pl.pallas_call(functools.partial(pack_kernel, element_count=element_count...  1 us
    pallas_call x1, Pallas kernels, on_device(): pl.pallas_call(functools.partial(evaluate_kernel, senders=senders, slots=...  0.81 us
    pallas_call x1, Pallas kernels, on_device(): pl.pallas_call(unpack_kernel, out_shape=jax.ShapeDtypeStruct((field_count...  0.75 us

profile of v4, /device:TPU:0, one launch (start us, length us, event | category | flops | bytes accessed | tf_op | source)
XLA Modules:
  0.0 25.9 jit_solution(1126859209334630363)
XLA Ops:
  0.0 1.0 %pack.1 = (f32[32,128]{1,0:T(8,128)S(1)}, bf16[128,1024]{1,0:T(8,128)(2,1)S(1)}) custom-call(f32[3,16,32]{2,1,0:T(8,128)} %bitcast.17, s32[16,32]{1,0:T(8,128)} %bitcast.18, s32[1,32]{1,0:T(1,128)} %counts_hbm.1, bf16[128,1024]{1,0:T(8,128)(2,1)} %bitcast.16), custom_call_target="tpu_custom_call" | custom-call | tf_op jit(solution)/shard_map/pack/pallas_call | solution.py:181
  1.0 14.4 %all_to_all.22 = f32[32,1,128]{2,1,0:T(1,128)S(1)} all-to-all(f32[32,1,128]{2,1,0:T(1,128)S(1)} %bitcast.15), channel_id=1, replica_groups=mesh['wide'=16,'narrow'=2] {'wide','narrow'}, dimensions={0} | all-to-all | bytes 32768 | tf_op jit(solution)/shard_map/all_to_all | solution.py:166
  15.4 0.8 %evaluate.1 = bf16[64,128]{1,0:T(8,128)(2,1)S(1)} custom-call(f32[32,128]{1,0:T(8,128)S(1)} %bitcast.12, bf16[128,1024]{1,0:T(8,128)(2,1)S(1)} %get-tuple-element.8.fields_ref), custom_call_target="tpu_custom_call" | custom-call | tf_op jit(solution)/shard_map/evaluate/pallas_call | solution.py:199
  16.2 8.9 %all_to_all.23 = bf16[32,2,128]{2,1,0:T(2,128)(2,1)S(1)} all-to-all(bf16[32,2,128]{2,1,0:T(2,128)(2,1)S(1)} %bitcast.13), channel_id=1, replica_groups=mesh['wide'=16,'narrow'=2] {'wide','narrow'}, dimensions={0} | all-to-all | bytes 32768 | tf_op jit(solution)/shard_map/all_to_all | solution.py:166
  25.1 0.8 %unpack.1 = bf16[16,16,32]{2,1,0:T(8,128)(2,1)} custom-call(bf16[64,128]{1,0:T(8,128)(2,1)S(1)} %bitcast.14), custom_call_target="tpu_custom_call" | custom-call | tf_op jit(solution)/shard_map/unpack/pallas_call | solution.py:212
